TPU v7x, 128 devices: a whole 4x4x4 slice. The times are simulated.
128 devices in a mesh: blk: 8 (over x, y_lo), uly: 2 (over core), dp: 8 (over z, y_hi).
Axes of the slice: x: 4, y: 4 (y_hi: 2, y_lo: 2; y = y_hi * 2 + y_lo), z: 4, core: 2. Of those that a mesh axis runs over, the one named last changes fastest.
Arguments:
- short_tokens: bfloat16 [64, 1024, 4096], P(('blk', 'dp'), 'uly'), may hold values from -150 to 150, as said below
- short_segments: int32 [64, 1024], P(('blk', 'dp')), may hold values from 0 to 3, never falling along the last dimension, each value on 1 to 512 neighbouring positions
- long_tokens: bfloat16 [8, 3072, 4096], P('dp', 'blk'), may hold values from -150 to 150, as said below
- long_lengths: int32 [8], P('dp'), may hold values from 768 to 3072
- w_query: bfloat16 [4096, 2048], P(('blk', 'dp'), 'uly'), may hold values from -0.09375 to 0.09375
- w_key: bfloat16 [4096, 512], P(('blk', 'dp'), 'uly'), may hold values from -0.09375 to 0.09375
- w_value: bfloat16 [4096, 512], P(('blk', 'dp'), 'uly'), may hold values from -0.09375 to 0.09375
Outputs:
- short_out: bfloat16 [64, 1024, 2048], P(('blk', 'dp'), 'uly')
- long_out: bfloat16 [8, 3072, 2048], P('dp', 'blk', 'uly')
Inputs may be any that keep to these rules, and one draw needn't show every extreme that they name: `short_tokens`: activations of the short bucket. `long_tokens`: activations of the long bucket; rows at or after a sequence's length are padding. `short_segments`: document numbers never fall along a sequence. `long_lengths`: a long sequence occupies positions 0 to its length - 1 of its 3072 slots.
All inputs are finite; a program needn't handle non-finite values.
Results may differ from a plain program's by a relative error of at most 0.012.
The roundings to bfloat16 on the way count: a program that leaves them out, or rounds other values in their place, can miss the bound.
Values may be sent and summed in bfloat16 or wider, within the bound.
A program may use at most 128 MiB of HBM per device.

v0:
```python
import math

import jax
import jax.numpy as jnp
from jax import lax
from jax.sharding import PartitionSpec as P

HD = 128


masked_score = -1e30


def side_by_side(arrays, axis, dim, along):
    both = jnp.concatenate(arrays, axis=along)
    whole, at, outs = (lax.all_gather(both, axis, axis=dim, tiled=True), 0, [])
    for a in arrays:
        outs.append(lax.slice_in_dim(whole, at, at + a.shape[along], axis=along))
        at += a.shape[along]
    return tuple(outs)


def head_scores(query_rows, key_rows, kv_heads):
    query_heads = query_rows.reshape(query_rows.shape[0], kv_heads, -1, HD)
    key_heads = key_rows.reshape(key_rows.shape[0], kv_heads, HD)
    scores = jnp.einsum(
        "bhgd,khd->hgbk", query_heads, key_heads, preferred_element_type=jnp.float32
    )
    return scores * (1.0 / math.sqrt(HD))


def weighted_values(probabilities, value_rows, kv_heads):
    value_heads = value_rows.reshape(value_rows.shape[0], kv_heads, HD)
    return jnp.einsum(
        "hgbk,khd->hgbd", probabilities, value_heads, preferred_element_type=jnp.float32
    )


def short_attention(queries, key_rows, value_rows, segments):
    kv_heads = key_rows.shape[1] // HD
    seq_len = key_rows.shape[0]
    block_rows = min(512, seq_len)
    positions = jnp.arange(seq_len, dtype=jnp.int32)
    outputs = []
    for block_index in range(seq_len // block_rows):
        first_row = block_index * block_rows
        query_pos = positions[first_row : first_row + block_rows]
        query_seg = segments[first_row : first_row + block_rows]
        visible = (positions[None, :] <= query_pos[:, None]) & (
            segments[None, :] == query_seg[:, None]
        )
        scores = head_scores(queries[first_row : first_row + block_rows], key_rows, kv_heads)
        scores = jnp.where(visible, scores, masked_score)
        row_max = jnp.max(scores, axis=-1, keepdims=True)
        exponentials = jnp.where(visible, jnp.exp(scores - row_max), 0.0)
        totals = jnp.sum(exponentials, axis=-1)
        mixed = (
            weighted_values(exponentials.astype(jnp.bfloat16), value_rows, kv_heads)
            / totals[..., None]
        )
        outputs.append(jnp.transpose(mixed, (2, 0, 1, 3)).reshape(block_rows, -1))
    return jnp.concatenate(outputs, axis=0).astype(jnp.bfloat16)


def local(short_tokens, short_segments, long_tokens, long_lengths, w_query, w_key, w_value):
    short_rows = short_tokens[0]
    long_rows = long_tokens[0]
    long_count = long_rows.shape[0]
    query_cols = w_query.shape[1]
    kv_cols = w_key.shape[1]
    whole_rows = lax.all_gather(short_rows, "uly", axis=0, tiled=True)
    pieces = side_by_side((w_query, w_key, w_value), ("blk", "dp"), 0, 1)
    short_new = tuple(
        (jnp.dot(whole_rows, pieces[i], preferred_element_type=jnp.float32) for i in range(3))
    )
    long_new = tuple(
        (jnp.dot(long_rows, pieces[i], preferred_element_type=jnp.float32) for i in range(3))
    )
    projected = short_new + long_new
    query_short, key_short, value_short = tuple(
        (item.astype(jnp.bfloat16) for item in projected[:3])
    )
    query_long, key_long, value_long = tuple((item.astype(jnp.bfloat16) for item in projected[3:]))
    attended = short_attention(query_short, key_short, value_short, short_segments[0])
    short_back = lax.all_to_all(attended, "uly", split_axis=0, concat_axis=1, tiled=True)
    long_len = long_lengths[0]
    query_pos = lax.axis_index("blk") * long_count + jnp.arange(long_count, dtype=jnp.int32)
    kv_heads = kv_cols // HD
    group_size = query_cols // kv_cols
    cycle_init = (
        jnp.full((kv_heads, group_size, long_count), masked_score, jnp.float32),
        jnp.zeros((kv_heads, group_size, long_count), jnp.float32),
        jnp.zeros((kv_heads, group_size, long_count, HD), jnp.float32),
    )
    carry = cycle_init
    key_piece, value_piece = side_by_side((key_long, value_long), "blk", 0, 1)
    piece_rows = key_piece.shape[0]
    block_rows = math.gcd(piece_rows, 512)
    blocks_count = piece_rows // block_rows
    key_blocks = key_piece.reshape(blocks_count, block_rows, -1)
    value_blocks = value_piece.reshape(blocks_count, block_rows, -1)
    block_starts = block_rows * jnp.arange(blocks_count, dtype=jnp.int32)

    def update(states, block_key, block_value, block_start):
        running_max, running_sum, accumulated = states
        key_pos = block_start + jnp.arange(block_rows, dtype=jnp.int32)
        visible = (key_pos[None, :] <= query_pos[:, None]) & (key_pos[None, :] < long_len)
        scores = jnp.where(visible, head_scores(query_long, block_key, kv_heads), masked_score)
        new_max = jnp.maximum(running_max, jnp.max(scores, axis=-1))
        rescale = jnp.exp(running_max - new_max)
        exponentials = jnp.where(visible, jnp.exp(scores - new_max[..., None]), 0.0)
        running_sum = running_sum * rescale + jnp.sum(exponentials, axis=-1)
        accumulated = accumulated * rescale[..., None] + weighted_values(
            exponentials.astype(jnp.bfloat16), block_value, kv_heads
        )
        return (new_max, running_sum, accumulated)

    def advance(states, inputs):
        block_key, block_value, block_start = inputs
        needed = (block_start <= query_pos[-1]) & (block_start < long_len)
        states = lax.cond(
            needed,
            lambda current: update(current, block_key, block_value, block_start),
            lambda current: current,
            states,
        )
        return (states, None)

    carry, unused = lax.scan(advance, carry, (key_blocks, value_blocks, block_starts))
    running_max, running_sum, accumulated = carry
    mixed = accumulated / running_sum[..., None]
    mixed = jnp.transpose(mixed, (2, 0, 1, 3)).reshape(long_count, query_cols)
    mixed = jnp.where(query_pos[:, None] < long_len, mixed, 0.0)
    return (short_back[None], mixed.astype(jnp.bfloat16)[None])


def solution(mesh):
    return jax.shard_map(
        local,
        mesh=mesh,
        in_specs=(
            P(("blk", "dp"), "uly", None),
            P(("blk", "dp"), None),
            P("dp", "blk", None),
            P("dp"),
            P(("blk", "dp"), "uly"),
            P(("blk", "dp"), "uly"),
            P(("blk", "dp"), "uly"),
        ),
        out_specs=(P(("blk", "dp"), "uly", None), P("dp", "blk", "uly")),
        check_vma=False,
    )
```

profile of v0, /device:TPU:39, one launch (start us, length us, event | category | flops | bytes accessed | tf_op | source)
XLA Modules:
  0.0 606.3 jit_solution(7188982247814746928)
XLA Ops:
  11.3 2.6 fusion.47
  13.9 298.6 %all-gather.5.cloned.1.call-done = bf16[4096,1536]{1,0:T(8,128)(2,1)} async-done(((bf16[64,1536]{1,0:T(8,128)(2,1)}), bf16[4096,1536]{1,0:T(8,128)(2,1)}) %all-gather.5.cloned.1.call-update) | async-done | bytes 12582928 | tf_op jit(solution)/shard_map/all_gather | solution.py:16
  312.5 2.9 fusion.91
  315.3 2.9 fusion.96
  319.1 76.5 %all-gather.9.cloned.1.call-done = bf16[1,1024,4096]{2,1,0:T(8,128)(2,1)} async-done(((bf16[1,512,4096]{2,1,0:T(8,128)(2,1)}), bf16[1,1024,4096]{2,1,0:T(8,128)(2,1)}) %all-gather.9.cloned.1.call-update) | async-done | bytes 8388624 | tf_op jit(solution)/shard_map/all_gather | solution.py:71
  395.6 7.4 %fusion.76 = bf16[256,1024]{1,0:T(8,128)(2,1)} fusion(bf16[1,1024,4096]{2,1,0:T(8,128)(2,1)} %all-gather.9.cloned.1.call-done, bf16[4096,1536]{1,0:T(8,128)(2,1)} %all-gather.5.cloned.1.call-done), kind=kOutput, calls=%fused_computation.73 | convolution fusion | flops 2147745792 | bytes 11010048 | tf_op jit(solution)/shard_map/dot_general | solution.py:74
  402.9 11.5 %convert_bitcast_fusion = bf16[1024,1024]{0,1:T(8,128)(2,1)S(1)} fusion(bf16[1,1024,4096]{2,1,0:T(8,128)(2,1)S(1)} %copy-done.3, bf16[4096,1536]{1,0:T(8,128)(2,1)} %all-gather.5.cloned.1.call-done), kind=kOutput, calls=%fused_computation.60 | convolution fusion | flops 8590983168 | bytes 18874368 | tf_op jit(solution)/shard_map/dot_general | solution.py:74
  414.4 5.0 fusion.71
  420.9 12.3 %fusion.108 = (f32[2,4,512]{2,1,0:T(4,128)S(1)}, bf16[2,4,512,1024]{2,3,1,0:T(8,128)(2,1)}) fusion(bf16[1024,2,128,1]{0,2,3,1:T(8,128)(2,1)} %bitcast.174, bf16[512,2,4,128]{0,3,2,1:T(8,128)(2,1)} %bitcast.164, pred[512,1024]{0,1:T(8,128)(4,1)} %get-tuple-element.220), kind=kOutput, calls=%fused_computation.90 | convolution fusion | flops 1098908672 | bytes 10502144 | tf_op jit(solution)/shard_map/sub | solution.py:55
  433.3 5.9 fusion.45
  439.1 12.1 %fusion.109 = (f32[2,4,512]{2,1,0:T(4,128)S(1)}, bf16[2,4,512,1024]{2,3,1,0:T(8,128)(2,1)}) fusion(bf16[1024,2,128,1]{0,2,3,1:T(8,128)(2,1)} %bitcast.175, bf16[512,2,4,128]{0,3,2,1:T(8,128)(2,1)} %bitcast.162, pred[512,1024]{0,1:T(8,128)(4,1)} %get-tuple-element.219), kind=kOutput, calls=%fused_computation.91 | convolution fusion | flops 1098908672 | bytes 10502144 | tf_op jit(solution)/shard_map/sub | solution.py:55
  451.3 5.0 fusion.46
  457.8 4.0 copy.66
  461.8 8.6 %all_to_all.13 = bf16[2,512,1024]{2,1,0:T(8,128)(2,1)} all-to-all(bf16[2,512,1024]{2,1,0:T(8,128)(2,1)} %bitcast.154), channel_id=1, replica_groups=mesh['blk'=8,'uly'=2,'dp'=8] {'uly'}, dimensions={0} | all-to-all | bytes 4194304 | tf_op jit(solution)/shard_map/all_to_all | solution.py:85
  470.4 4.0 copy.67
  474.3 3.9 copy.74
  478.2 7.9 %fusion.66 = bf16[384,1024]{0,1:T(8,128)(2,1)} fusion(bf16[1,384,4096]{2,1,0:T(8,128)(2,1)S(1)} %copy-done, bf16[4096,1536]{1,0:T(8,128)(2,1)} %all-gather.5.cloned.1.call-done), kind=kOutput, calls=%fused_computation.71 | convolution fusion | flops 3221618688 | bytes 12320768 | tf_op jit(solution)/shard_map/dot_general | solution.py:77
  487.6 3.7 fusion.105
  499.2 92.0 %while.14 = (s32[]{:T(128)}, f32[2,4,384]{2,1,0:T(4,128)S(1)}, f32[2,4,384]{2,1,0:T(4,128)S(1)}, f32[2,4,384,128]{3,2,1,0:T(8,128)}, s32[6]{0:T(128)S(1)}, /*ind...) while((s32[]{:T(128)}, f32[2,4,384]{2,1,0:T(4,128)S(1)}, ...), condition=%wide.region_9.10_spmd, body=%wide.region_4.9_spmd.sunk | while | flops 826940928 | bytes 26942268 | solution.py:129
  503.0 11.5 %conditional.2 = ((f32[2,4,384]{2,1,0:T(4,128)S(1)}, f32[2,4,384]{2,1,0:T(4,128)S(1)}, f32[2,4,384,128]{3,2,1,0:T(8,128)})) conditional(s32[]{:T(128)} %convert_element_type.107, (f32[2,4,384]{2,1,0:T(4,128)S(1)}, f32[2,4,384]{2,1,0:T(4,128)S(1)}, f32[2,4,384,128]{3,2,1,0:T(8,128)}) %tuple.52, (s32[]{:T(128)}, s32[384]{0:T(512)S(1)}, s32[]{:T(128)}, ...), branch_computations={%region_5.5_spmd, %region_6.8_spmd} | conditional | flops 826940928 | bytes 26942000 | solution.py:121
  509.8 4.7 multiply_add_fusion
  518.4 11.5 %conditional.2 = ((f32[2,4,384]{2,1,0:T(4,128)S(1)}, f32[2,4,384]{2,1,0:T(4,128)S(1)}, f32[2,4,384,128]{3,2,1,0:T(8,128)})) conditional(s32[]{:T(128)} %convert_element_type.107, (f32[2,4,384]{2,1,0:T(4,128)S(1)}, f32[2,4,384]{2,1,0:T(4,128)S(1)}, f32[2,4,384,128]{3,2,1,0:T(8,128)}) %tuple.52, (s32[]{:T(128)}, s32[384]{0:T(512)S(1)}, s32[]{:T(128)}, ...), branch_computations={%region_5.5_spmd, %region_6.8_spmd} | conditional | flops 826940928 | bytes 26942000 | solution.py:121
  525.2 4.7 multiply_add_fusion
  533.7 11.5 %conditional.2 = ((f32[2,4,384]{2,1,0:T(4,128)S(1)}, f32[2,4,384]{2,1,0:T(4,128)S(1)}, f32[2,4,384,128]{3,2,1,0:T(8,128)})) conditional(s32[]{:T(128)} %convert_element_type.107, (f32[2,4,384]{2,1,0:T(4,128)S(1)}, f32[2,4,384]{2,1,0:T(4,128)S(1)}, f32[2,4,384,128]{3,2,1,0:T(8,128)}) %tuple.52, (s32[]{:T(128)}, s32[384]{0:T(512)S(1)}, s32[]{:T(128)}, ...), branch_computations={%region_5.5_spmd, %region_6.8_spmd} | conditional | flops 826940928 | bytes 26942000 | solution.py:121
  540.5 4.7 multiply_add_fusion
  549.0 11.5 %conditional.2 = ((f32[2,4,384]{2,1,0:T(4,128)S(1)}, f32[2,4,384]{2,1,0:T(4,128)S(1)}, f32[2,4,384,128]{3,2,1,0:T(8,128)})) conditional(s32[]{:T(128)} %convert_element_type.107, (f32[2,4,384]{2,1,0:T(4,128)S(1)}, f32[2,4,384]{2,1,0:T(4,128)S(1)}, f32[2,4,384,128]{3,2,1,0:T(8,128)}) %tuple.52, (s32[]{:T(128)}, s32[384]{0:T(512)S(1)}, s32[]{:T(128)}, ...), branch_computations={%region_5.5_spmd, %region_6.8_spmd} | conditional | flops 826940928 | bytes 26942000 | solution.py:121
  555.9 4.7 multiply_add_fusion
  564.4 11.5 %conditional.2 = ((f32[2,4,384]{2,1,0:T(4,128)S(1)}, f32[2,4,384]{2,1,0:T(4,128)S(1)}, f32[2,4,384,128]{3,2,1,0:T(8,128)})) conditional(s32[]{:T(128)} %convert_element_type.107, (f32[2,4,384]{2,1,0:T(4,128)S(1)}, f32[2,4,384]{2,1,0:T(4,128)S(1)}, f32[2,4,384,128]{3,2,1,0:T(8,128)}) %tuple.52, (s32[]{:T(128)}, s32[384]{0:T(512)S(1)}, s32[]{:T(128)}, ...), branch_computations={%region_5.5_spmd, %region_6.8_spmd} | conditional | flops 826940928 | bytes 26942000 | solution.py:121
  571.2 4.7 multiply_add_fusion
  579.7 11.5 %conditional.2 = ((f32[2,4,384]{2,1,0:T(4,128)S(1)}, f32[2,4,384]{2,1,0:T(4,128)S(1)}, f32[2,4,384,128]{3,2,1,0:T(8,128)})) conditional(s32[]{:T(128)} %convert_element_type.107, (f32[2,4,384]{2,1,0:T(4,128)S(1)}, f32[2,4,384]{2,1,0:T(4,128)S(1)}, f32[2,4,384,128]{3,2,1,0:T(8,128)}) %tuple.52, (s32[]{:T(128)}, s32[384]{0:T(512)S(1)}, s32[]{:T(128)}, ...), branch_computations={%region_5.5_spmd, %region_6.8_spmd} | conditional | flops 826940928 | bytes 26942000 | solution.py:121
  586.5 4.7 multiply_add_fusion
  594.8 2.3 reshape.130
  (110 shorter events, 70.0 us)
Async XLA Ops:
  7.2 305.3 %copy-start = (bf16[1,384,4096]{2,1,0:T(8,128)(2,1)S(1)}, bf16[1,384,4096]{2,1,0:T(8,128)(2,1)}, u32[]{:S(2)}) copy-start(bf16[1,384,4096]{2,1,0:T(8,128)(2,1)} %param.13) | copy-start | bytes 9437188
  7.2 305.3 %all-gather.5.cloned.1.call-start = ((), (), s32[]{:S(2)}) async-start(), calls=%async_computation.1 | async-start | bytes 12779520 | tf_op jit(solution)/shard_map/all_gather | solution.py:16
  9.0 386.6 %all-gather.9.cloned.1.call-start = ((), (), s32[]{:S(2)}) async-start(), calls=%async_computation.3 | async-start | bytes 12582912 | tf_op jit(solution)/shard_map/all_gather | solution.py:71
  9.8 477.8 %all-gather.7.cloned.1.call-start = ((), (), s32[]{:S(2)}) async-start(), calls=%async_computation.2 | async-start | bytes 3538944 | tf_op jit(solution)/shard_map/all_gather | solution.py:16
  395.6 7.4 %copy-start.3 = (bf16[1,1024,4096]{2,1,0:T(8,128)(2,1)S(1)}, bf16[1,1024,4096]{2,1,0:T(8,128)(2,1)}, u32[]{:S(2)}) copy-start(bf16[1,1024,4096]{2,1,0:T(8,128)(2,1)} %all-gather.9.cloned.1.call-done) | copy-start | bytes 25165828
  451.2 5.0 copy-start.2
  591.3 8.1 %copy-start.1 = (bf16[1,384,4096]{2,1,0:T(8,128)(2,1)S(1)}, bf16[1,384,4096]{2,1,0:T(8,128)(2,1)}, u32[]{:S(2)}) copy-start(bf16[1,384,4096]{2,1,0:T(8,128)(2,1)} %param.13) | copy-start | bytes 9437188
Sparse Core Ops, SparseCore 0:
  10.2 302.1 all-gather.4
  314.1 81.4 all-gather.8
  397.2 70.6 all-gather.6
where the time goes:
time: 613 us; the launch traced here: 606 us
  waiting for transfers between devices  376 us (61%)
  matrix products  109 us (18%)
  local copies, waits for them, and re-layouts  48 us (8%)
  other arithmetic  33.8 us (6%)
  loops' own time  15.9 us (3%)
  between operations  15 us (2%)
  blocking collectives  8.59 us (1%)
    all_gather x2, waiting for transfers between devices, side_by_side(): whole, at, outs = (lax.all_gather(both, axis, axis=dim, tiled=True), 0, [])  299 us
    all_gather x1, waiting for transfers between devices, local(): whole_rows = lax.all_gather(short_rows, 'uly', axis=0, tiled=True)  76.5 us
    dot_general x8, matrix products, weighted_values(): jnp.einsum('hgbk,khd->hgbd', probabilities, value_heads, preferred_elemen...  39.2 us
    sub x2, matrix products, short_attention(): exponentials = jnp.where(visible, jnp.exp(scores - row_max), 0.0)  24.5 us
    dot_general x3, matrix products, local(): jnp.dot(whole_rows, pieces[i], preferred_element_type=jnp.float32)  23.8 us
    another operation x1, loops' own time, local(): lax.scan(advance, carry, (key_blocks, value_blocks, block_starts))  15.5 us
    dot_general x3, matrix products, local(): jnp.dot(long_rows, pieces[i], preferred_element_type=jnp.float32)  13.7 us
  transfers between devices with their start and end apart: 3, of which 2 were waited for; matrix products, arithmetic and copies ran while one was open for 15% of the time, Pallas kernels for 0%

commit v1 on v0

v1 whole, which is shorter than its diff:
```python
import math

import jax
import jax.numpy as jnp
from jax import lax
from jax.experimental import pallas as pl
from jax.experimental.pallas import tpu as pltpu
from jax.sharding import PartitionSpec as P

MESH = pl.DeviceIdType.MESH
BF16 = jnp.bfloat16
F32 = jnp.float32
HD = 128
D = 4096
SEQ = 1024
HALF = 512
LONG = 384
ROWS = SEQ + LONG
GROUPS = 6
WIDTH = 256
HIDDEN = -1e30
SCALE = math.log2(math.e) / math.sqrt(HD)

PARTS = ((0, 32, "xyz"), (32, 16, "yzx"), (48, 16, "zxy"))

NT = (((1,), (1,)), ((), ()))


def kernel(
    xs_hbm, seg_ref, xl_hbm, len_ref, wq_hbm, wk_hbm, wv_hbm,
    so_hbm, lo_hbm,
    w, x, kb, vb, qb, kvl, sob, lob, bias_s, bias_l, q2, acc, mx, tot,
    send_sem, recv_sem, kv_send, kv_recv, x_sem, own_sem, out_send, out_recv, out_own,
):
    blk, core, dp = lax.axis_index("blk"), lax.axis_index("uly"), lax.axis_index("dp")
    cx, yl = blk // 2, blk % 2
    cz, yh = dp // 2, dp % 2
    cy = yh * 2 + yl
    here = {"x": cx, "y": cy, "z": cz}

    def device(dim, step):
        at = dict(here)
        at[dim] = (here[dim] + step + 4) % 4
        return (at["x"] * 2 + at["y"] % 2, core, at["z"] * 2 + at["y"] // 2)

    sibling = (blk, 1 - core, dp)

    own = [
        pltpu.make_async_copy(wk_hbm, w.at[0, cx, yl, cz, yh], own_sem.at[0]),
        pltpu.make_async_copy(wv_hbm, w.at[1, cx, yl, cz, yh], own_sem.at[1]),
    ]
    for g in range(4):
        own.append(
            pltpu.make_async_copy(
                wq_hbm.at[:, pl.ds(g * WIDTH, WIDTH)], w.at[2 + g, cx, yl, cz, yh], own_sem.at[2 + g]
            )
        )
    my_rows = pl.ds(pl.multiple_of(core * HALF, HALF), HALF)
    own_x = pltpu.make_async_copy(xs_hbm.at[0], x.at[my_rows], x_sem.at[0])
    own_l = pltpu.make_async_copy(xl_hbm.at[0], x.at[pl.ds(SEQ, LONG)], x_sem.at[1])
    for copy in own + [own_l, own_x]:
        copy.start()

    barrier = pltpu.get_barrier_semaphore()
    for dim in "xyz":
        for step in (1, -1):
            pl.semaphore_signal(barrier, inc=1, device_id=device(dim, step), device_id_type=MESH)
    pl.semaphore_signal(barrier, inc=1, device_id=sibling, device_id_type=MESH)
    pl.semaphore_wait(barrier, 7)

    peer_x = pltpu.make_async_remote_copy(
        src_ref=xs_hbm.at[0], dst_ref=x.at[my_rows], send_sem=x_sem.at[2], recv_sem=x_sem.at[3],
        device_id=sibling, device_id_type=MESH,
    )
    for copy in own:
        copy.wait()

    def block(groups, part, phase, position, half=None):
        first, count, order = PARTS[part]
        dim = order[phase]
        at = dict(here)
        at[dim] = position
        done = order[:phase]
        ix = slice(None) if "x" in done else at["x"]
        iz = slice(None) if "z" in done else at["z"]
        il = slice(None) if "y" in done else at["y"] % 2
        ih = slice(None) if "y" in done else at["y"] // 2
        columns = slice(None)
        if half is not None:
            if phase == 0:
                columns = pl.ds(half * 128, 128)
            elif order[0] == "x":
                ix = pl.ds(2 * half, 2)
            elif order[0] == "z":
                iz = pl.ds(2 * half, 2)
            else:
                il = half
        return w.at[groups, ix, il, iz, ih, pl.ds(first, count), columns]

    def hop(groups, stage, part, phase, slot):
        dim = PARTS[part][2][phase]
        step = 1 if slot % 2 == 0 else -1
        if slot < 2:
            ref = block(groups, part, phase, here[dim])
        else:
            ref = block(groups, part, phase, (here[dim] - step + 4) % 4, half=slot % 2)
        return pltpu.make_async_remote_copy(
            src_ref=ref, dst_ref=ref,
            send_sem=send_sem.at[stage, part, slot], recv_sem=recv_sem.at[stage, part, slot],
            device_id=device(dim, step), device_id_type=MESH,
        )

    sent = []

    def send(phase, g, second):
        groups = slice(None) if phase == 0 else g
        stage = 0 if phase == 0 else 1 + (phase - 1) * GROUPS + g
        for part in range(3):
            for slot in (2, 3) if second else (0, 1):
                copy = hop(groups, stage, part, phase, slot)
                copy.start()
                sent.append(copy)

    def arrive(phase, g, second):
        groups = slice(None) if phase == 0 else g
        stage = 0 if phase == 0 else 1 + (phase - 1) * GROUPS + g
        for part in range(3):
            for slot in (2, 3) if second else (0, 1):
                hop(groups, stage, part, phase, slot).wait_recv()

    def kv_copy(index, ref, dim, step):
        return pltpu.make_async_remote_copy(
            src_ref=ref, dst_ref=ref, send_sem=kv_send.at[index], recv_sem=kv_recv.at[index],
            device_id=device(dim, step) if dim == "x" else ((cx * 2 + 1 - yl), core, dp), device_id_type=MESH,
        )

    def kv_hops(index):
        left, right = (cx + 3) % 4, (cx + 1) % 4
        if index == 0:
            return kv_copy(0, kvl.at[cx, yl, pl.ds(0, 2)], "y", 0)
        if index in (1, 2):
            return kv_copy(index, kvl.at[cx, yl, pl.ds(2, 2)], "x", 1 if index == 1 else -1)
        if index in (3, 4):
            return kv_copy(index, kvl.at[cx, :, pl.ds(0, 2)], "x", 1 if index == 3 else -1)
        if index == 5:
            return kv_copy(5, kvl.at[left, yl, 2], "x", 1)
        if index == 6:
            return kv_copy(6, kvl.at[right, yl, 3], "x", -1)
        if index == 7:
            return kv_copy(7, kvl.at[left, 0, pl.ds(0, 2)], "x", 1)
        if index == 8:
            return kv_copy(8, kvl.at[right, 1, pl.ds(0, 2)], "x", -1)
        return kv_copy(9, kvl.at[:, yl, pl.ds(2, 2)], "y", 0)

    def kv_start(*indices):
        for index in indices:
            copy = kv_hops(index)
            copy.start()
            sent.append(copy)

    def kv_wait(*indices):
        for index in indices:
            kv_hops(index).wait_recv()

    def project(g, out):
        tile = 352

        @pl.loop(0, ROWS // tile)
        def _(i):
            rows = pl.ds(pl.multiple_of(i * tile, 32), tile)
            out[rows, :] = jnp.dot(
                x[rows, :], w[g].reshape(D, WIDTH), preferred_element_type=F32
            ).astype(BF16)

    def short_bias():
        @pl.loop(0, 8)
        def _(i):
            first = pl.multiple_of(i * 128, 128)
            own_seg = seg_ref[:, pl.ds(first, 128)].astype(F32)
            query_seg = jnp.transpose(jnp.broadcast_to(own_seg, (128, 128)))
            window = jnp.maximum(i // 2 - 2, 0) * 256
            for j in range(6):
                start = pl.multiple_of(window + j * 128, 128)
                key_seg = jnp.broadcast_to(seg_ref[:, pl.ds(start, 128)].astype(F32), (128, 128))
                query_pos = first + lax.broadcasted_iota(jnp.int32, (128, 128), 0)
                key_pos = start + lax.broadcasted_iota(jnp.int32, (128, 128), 1)
                visible = (key_pos <= query_pos) & (key_seg == query_seg)
                bias_s[pl.ds(first, 128), pl.ds(j * 128, 128)] = jnp.where(visible, 0.0, HIDDEN)

    def long_bias():
        query_pos = lax.broadcasted_iota(jnp.int32, (LONG, LONG), 0)
        key_pos = lax.broadcasted_iota(jnp.int32, (LONG, LONG), 1)
        visible = (key_pos <= query_pos) & (key_pos + blk * LONG < len_ref[0])
        bias_l[...] = jnp.where(visible, 0.0, HIDDEN)

    def short_attention(g):
        kv = pl.ds((g // 2) * HD, HD)
        for i in range(4):
            keys = pl.ds(max(i - 2, 0) * 256, 256 * min(i + 1, 3))
            rows = pl.ds(i * 256, 256)
            for h in range(2):
                scores = lax.dot_general(
                    qb[g, rows, pl.ds(h * HD, HD)], kb[keys, kv], NT, preferred_element_type=F32
                )
                scores = scores * SCALE + bias_s[rows, pl.ds(0, 256 * min(i + 1, 3))]
                top = jnp.max(scores, axis=1, keepdims=True)
                weights = jnp.exp2(scores - top)
                total = jnp.sum(weights, axis=1, keepdims=True)
                mixed = jnp.dot(weights.astype(BF16), vb[keys, kv], preferred_element_type=F32)
                sob[g, rows, pl.ds(h * HD, HD)] = (mixed / total).astype(BF16)

    def long_step(kv, j, bias, fresh):
        keys = kvl[j // 2, j % 2, 2 * kv]
        values = kvl[j // 2, j % 2, 2 * kv + 1]
        scores = lax.dot_general(q2[...], keys, NT, preferred_element_type=F32) * SCALE + bias
        top = jnp.maximum(mx[...], jnp.max(scores, axis=1, keepdims=True))
        shrink = jnp.exp2(mx[...] - top)
        weights = jnp.exp2(scores - top)
        tot[...] = tot[...] * shrink + jnp.sum(weights, axis=1, keepdims=True)
        acc[...] = acc[...] * shrink + jnp.dot(
            weights.astype(BF16), values, preferred_element_type=F32
        )
        mx[...] = top

    def long_attention(g):
        kv = g // 2
        length = len_ref[0]
        q2[pl.ds(0, LONG), :] = qb[g, pl.ds(SEQ, LONG), pl.ds(0, HD)]
        q2[pl.ds(LONG, LONG), :] = qb[g, pl.ds(SEQ, LONG), pl.ds(HD, HD)]
        mx[...] = jnp.full_like(mx, HIDDEN)
        tot[...] = jnp.zeros_like(tot)
        acc[...] = jnp.zeros_like(acc)

        @pl.loop(0, blk)
        def _(j):
            key_pos = j * LONG + lax.broadcasted_iota(jnp.int32, (1, LONG), 1)
            long_step(kv, j, jnp.where(key_pos < length, 0.0, HIDDEN), False)

        diagonal = bias_l[...]
        long_step(kv, blk, jnp.concatenate([diagonal, diagonal], axis=0), False)
        query_pos = blk * LONG + lax.broadcasted_iota(jnp.int32, (LONG, HD), 0)
        for h in range(2):
            half = pl.ds(h * LONG, LONG)
            mixed = acc[half, :] / tot[half, :]
            lob[g, :, pl.ds(h * HD, HD)] = jnp.where(query_pos < length, mixed, 0.0).astype(BF16)

    outs = []
    peer_outs = []

    def ship_short(g):
        columns = pl.ds(pl.multiple_of(core * SEQ + g * WIDTH, WIDTH), WIDTH)
        theirs = pl.ds(pl.multiple_of((1 - core) * HALF, HALF), HALF)
        peer = pltpu.make_async_remote_copy(
            src_ref=sob.at[g, theirs], dst_ref=so_hbm.at[0, :, columns],
            send_sem=out_send.at[g], recv_sem=out_recv.at[g], device_id=sibling, device_id_type=MESH,
        )
        mine = pltpu.make_async_copy(sob.at[g, my_rows], so_hbm.at[0, :, columns], out_own.at[g])
        peer.start()
        mine.start()
        peer_outs.append(peer)
        outs.append(mine)

    def ship_long(g):
        mine = pltpu.make_async_copy(
            lob.at[g], lo_hbm.at[0, :, pl.ds(g * WIDTH, WIDTH)], out_own.at[4 + g]
        )
        mine.start()
        outs.append(mine)

    send(0, 0, False)
    peer_x.start()
    long_bias()
    arrive(0, 0, False)
    send(0, 0, True)
    short_bias()
    arrive(0, 0, True)
    send(1, 0, False)
    send(1, 1, False)
    own_x.wait()
    own_l.wait()
    arrive(1, 0, False)
    send(1, 0, True)
    arrive(1, 0, True)
    send(2, 0, False)
    arrive(1, 1, False)
    send(1, 1, True)
    send(1, 2, False)
    arrive(1, 1, True)
    send(2, 1, False)
    peer_x.wait_recv()

    def turn_one(g):
        if g + 2 < GROUPS:
            arrive(1, g + 2, False)
            send(1, g + 2, True)
        if g + 3 < GROUPS:
            send(1, g + 3, False)
        if g < GROUPS:
            arrive(2, g, False)
            send(2, g, True)

    def turn_two(g):
        if g + 2 < GROUPS:
            arrive(1, g + 2, True)
            send(2, g + 2, False)

    def turn_three(g):
        if g < GROUPS:
            arrive(2, g, True)

    turn_one(0)
    turn_two(0)
    turn_three(0)
    project(0, kb)
    turn_one(1)
    turn_two(1)
    turn_three(1)
    project(1, vb)
    for h in range(2):
        kvl[cx, yl, 2 * h] = kb[pl.ds(SEQ, LONG), pl.ds(h * HD, HD)]
        kvl[cx, yl, 2 * h + 1] = vb[pl.ds(SEQ, LONG), pl.ds(h * HD, HD)]
    turn_one(2)
    kv_start(0, 1, 2)
    turn_two(2)
    turn_three(2)
    project(2, qb.at[0])
    turn_one(3)
    kv_wait(0)
    kv_start(3, 4)
    kv_wait(1, 2)
    kv_start(5, 6)
    short_attention(0)
    ship_short(0)
    turn_two(3)
    kv_wait(5, 6)
    kv_start(9)
    kv_wait(3, 4)
    kv_start(7, 8)
    turn_three(3)
    project(3, qb.at[1])
    turn_one(4)
    short_attention(1)
    ship_short(1)
    kv_wait(7, 8)
    kv_wait(9)
    long_attention(0)
    ship_long(0)
    turn_three(4)
    project(4, qb.at[2])
    turn_one(5)
    short_attention(2)
    ship_short(2)
    long_attention(1)
    ship_long(1)
    turn_three(5)
    project(5, qb.at[3])
    short_attention(3)
    ship_short(3)
    long_attention(2)
    ship_long(2)
    long_attention(3)
    ship_long(3)

    peer_x.wait_send()
    for copy in sent:
        copy.wait_send()
    for copy in outs:
        copy.wait()
    for copy in peer_outs:
        copy.wait()


def local(short_tokens, short_segments, long_tokens, long_lengths, w_query, w_key, w_value):
    anywhere = pl.BlockSpec(memory_space=pl.ANY)
    vmem = pl.BlockSpec(memory_space=pltpu.VMEM)
    smem = pl.BlockSpec(memory_space=pltpu.SMEM)
    dma = pltpu.SemaphoreType.DMA
    return pl.pallas_call(
        kernel,
        out_shape=(
            jax.ShapeDtypeStruct((1, HALF, 2 * SEQ), BF16),
            jax.ShapeDtypeStruct((1, LONG, SEQ), BF16),
        ),
        in_specs=[anywhere, vmem, anywhere, smem, anywhere, anywhere, anywhere],
        out_specs=(anywhere, anywhere),
        scratch_shapes=[
            pltpu.VMEM((GROUPS, 4, 2, 4, 2, 64, WIDTH), BF16),
            pltpu.VMEM((ROWS, D), BF16),
            pltpu.VMEM((ROWS, WIDTH), BF16),
            pltpu.VMEM((ROWS, WIDTH), BF16),
            pltpu.VMEM((4, ROWS, WIDTH), BF16),
            pltpu.VMEM((4, 2, 4, LONG, HD), BF16),
            pltpu.VMEM((4, SEQ, WIDTH), BF16),
            pltpu.VMEM((4, LONG, WIDTH), BF16),
            pltpu.VMEM((SEQ, 768), F32),
            pltpu.VMEM((LONG, LONG), F32),
            pltpu.VMEM((2 * LONG, HD), BF16),
            pltpu.VMEM((2 * LONG, HD), F32),
            pltpu.VMEM((2 * LONG, 1), F32),
            pltpu.VMEM((2 * LONG, 1), F32),
            dma((13, 3, 4)),
            dma((13, 3, 4)),
            dma((10,)),
            dma((10,)),
            dma((4,)),
            dma((6,)),
            dma((4,)),
            dma((4,)),
            dma((8,)),
        ],
        compiler_params=pltpu.CompilerParams(
            collective_id=0, has_side_effects=True, vmem_limit_bytes=63_000_000
        ),
    )(short_tokens, short_segments, long_tokens, long_lengths, w_query, w_key, w_value)


def solution(mesh):
    return jax.shard_map(
        local,
        mesh=mesh,
        in_specs=(
            P(("blk", "dp"), "uly", None),
            P(("blk", "dp"), None),
            P("dp", "blk", None),
            P("dp"),
            P(("blk", "dp"), "uly"),
            P(("blk", "dp"), "uly"),
            P(("blk", "dp"), "uly"),
        ),
        out_specs=(P(("blk", "dp"), "uly", None), P("dp", "blk", "uly")),
        check_vma=False,
    )
```

time: 613 us -> 177 us (0.29)
  the two profiles are of different devices: /device:TPU:39 before, /device:TPU:14 now
where the time goes in v1:
time: 177 us
  Pallas kernels  171 us (97%)
  local copies, waits for them, and re-layouts  4.12 us (2%)
    pallas_call x1, Pallas kernels, local(): pl.pallas_call(kernel, out_shape=(jax.ShapeDtypeStruct((1, HALF, 2 * SEQ)...  171 us
    unnamed x4, local copies, waits for them, and re-layouts  4.12 us

profile of v1, /device:TPU:14, one launch (start us, length us, event | category | flops | bytes accessed | tf_op | source)
XLA Modules:
  0.0 176.5 jit_solution(1431096085614528317)
XLA Ops:
  1.3 171.1 %shard_map.86 = (bf16[1,512,2048]{2,1,0:T(8,128)(2,1)}, bf16[1,384,1024]{2,1,0:T(8,128)(2,1)}) custom-call(bf16[1,512,4096]{2,1,0:T(8,128)(2,1)} %xs_hbm.1, s32[1,1024]{1,0:T(1,128)} %seg_ref.1, bf16[1,384,4096]{2,1,0:T(8,128)(2,1)} %xl_hbm.1, s32[1]{0:T(128)S(6)} %copy.11.len_ref, bf16[64,1024]{1,0:T(8,128)(2,1)} %wq_hbm.1, bf16[64,256]{1,0:T(8,128)(2,1)} %wk_hbm.1, ...), custom_call_target="tpu_custom_call" | custom-call | tf_op jit(solution)/shard_map/pallas_call | solution.py:378
  172.4 0.0 copy-start
  172.4 3.2 %copy.12 = bf16[1,512,2048]{2,1,0:T(8,128)(2,1)} copy(bf16[1,512,2048]{2,1,0:T(8,128)(2,1)} %get-tuple-element.4) | data formatting | bytes 4194304
  175.6 0.0 copy-done
  175.6 0.9 copy.13
Async XLA Ops:
  172.4 3.2 %copy-start = (bf16[1,384,1024]{2,1,0:T(8,128)(2,1)S(1)}, bf16[1,384,1024]{2,1,0:T(8,128)(2,1)}, u32[]{:S(2)}) copy-start(bf16[1,384,1024]{2,1,0:T(8,128)(2,1)} %get-tuple-element.5) | copy-start | bytes 2359300

commit v2 on v1

--- a/solution.py
+++ b/solution.py
@@ -29,7 +29,7 @@
 def kernel(
     xs_hbm, seg_ref, xl_hbm, len_ref, wq_hbm, wk_hbm, wv_hbm,
     so_hbm, lo_hbm,
-    w, x, kb, vb, qb, kvl, sob, lob, bias_s, bias_l, q2, acc, mx, tot,
+    w, x, kb, vb, qb, kvl, sob, lob, bias_s, bias_l, sc_s, sc_l, acc, mx, tot,
     send_sem, recv_sem, kv_send, kv_recv, x_sem, own_sem, out_send, out_recv, out_own,
 ):
     blk, core, dp = lax.axis_index("blk"), lax.axis_index("uly"), lax.axis_index("dp")
@@ -163,11 +163,10 @@
             kv_hops(index).wait_recv()
 
     def project(g, out):
-        tile = 352
-
-        @pl.loop(0, ROWS // tile)
-        def _(i):
-            rows = pl.ds(pl.multiple_of(i * tile, 32), tile)
+        tile = 704
+
+        for i in range(ROWS // tile):
+            rows = pl.ds(i * tile, tile)
             out[rows, :] = jnp.dot(
                 x[rows, :], w[g].reshape(D, WIDTH), preferred_element_type=F32
             ).astype(BF16)
@@ -188,61 +187,115 @@
                 bias_s[pl.ds(first, 128), pl.ds(j * 128, 128)] = jnp.where(visible, 0.0, HIDDEN)
 
     def long_bias():
-        query_pos = lax.broadcasted_iota(jnp.int32, (LONG, LONG), 0)
-        key_pos = lax.broadcasted_iota(jnp.int32, (LONG, LONG), 1)
-        visible = (key_pos <= query_pos) & (key_pos + blk * LONG < len_ref[0])
+        query_pos = yl * LONG + lax.broadcasted_iota(jnp.int32, (LONG, 2 * LONG), 0)
+        key_pos = lax.broadcasted_iota(jnp.int32, (LONG, 2 * LONG), 1)
+        visible = (key_pos <= query_pos) & (key_pos + cx * (2 * LONG) < len_ref[0])
         bias_l[...] = jnp.where(visible, 0.0, HIDDEN)
 
     def short_attention(g):
         kv = pl.ds((g // 2) * HD, HD)
-        for i in range(4):
-            keys = pl.ds(max(i - 2, 0) * 256, 256 * min(i + 1, 3))
+        items = [(i, h) for i in range(4) for h in range(2)]
+
+        def score(n):
+            i, h = items[n]
+            width = 256 * min(i + 1, 3)
+            sc_s[n % 2, :, pl.ds(0, width)] = lax.dot_general(
+                qb[g, pl.ds(i * 256, 256), pl.ds(h * HD, HD)],
+                kb[pl.ds(max(i - 2, 0) * 256, width), kv],
+                NT,
+                preferred_element_type=F32,
+            )
+
+        score(0)
+        for n, (i, h) in enumerate(items):
+            if n + 1 < len(items):
+                score(n + 1)
+            width = 256 * min(i + 1, 3)
             rows = pl.ds(i * 256, 256)
-            for h in range(2):
-                scores = lax.dot_general(
-                    qb[g, rows, pl.ds(h * HD, HD)], kb[keys, kv], NT, preferred_element_type=F32
-                )
-                scores = scores * SCALE + bias_s[rows, pl.ds(0, 256 * min(i + 1, 3))]
-                top = jnp.max(scores, axis=1, keepdims=True)
-                weights = jnp.exp2(scores - top)
-                total = jnp.sum(weights, axis=1, keepdims=True)
-                mixed = jnp.dot(weights.astype(BF16), vb[keys, kv], preferred_element_type=F32)
-                sob[g, rows, pl.ds(h * HD, HD)] = (mixed / total).astype(BF16)
-
-    def long_step(kv, j, bias, fresh):
-        keys = kvl[j // 2, j % 2, 2 * kv]
-        values = kvl[j // 2, j % 2, 2 * kv + 1]
-        scores = lax.dot_general(q2[...], keys, NT, preferred_element_type=F32) * SCALE + bias
-        top = jnp.maximum(mx[...], jnp.max(scores, axis=1, keepdims=True))
-        shrink = jnp.exp2(mx[...] - top)
-        weights = jnp.exp2(scores - top)
-        tot[...] = tot[...] * shrink + jnp.sum(weights, axis=1, keepdims=True)
-        acc[...] = acc[...] * shrink + jnp.dot(
-            weights.astype(BF16), values, preferred_element_type=F32
-        )
-        mx[...] = top
+            scores = sc_s[n % 2, :, pl.ds(0, width)] * SCALE + bias_s[rows, pl.ds(0, width)]
+            top = jnp.max(scores, axis=1, keepdims=True)
+            weights = jnp.exp2(scores - top)
+            total = jnp.sum(weights, axis=1, keepdims=True)
+            mixed = jnp.dot(
+                weights.astype(BF16),
+                vb[pl.ds(max(i - 2, 0) * 256, width), kv],
+                preferred_element_type=F32,
+            )
+            sob[g, rows, pl.ds(h * HD, HD)] = (mixed / total).astype(BF16)
+
+    def tiles(value):
+        return [value[:, t * HD : (t + 1) * HD] for t in range(value.shape[1] // HD)]
+
+    def fold(op, value):
+        parts = tiles(value)
+        while len(parts) > 1:
+            parts = [
+                op(parts[n], parts[n + 1]) if n + 1 < len(parts) else parts[n]
+                for n in range(0, len(parts), 2)
+            ]
+        return parts[0]
+
+    def pair(j, which):
+        return jnp.concatenate([kvl[j, 0, which], kvl[j, 1, which]], axis=0)
+
+    def long_score(g, h, j, bias):
+        scores = bias + lax.dot_general(
+            qb[g, pl.ds(SEQ, LONG), pl.ds(h * HD, HD)],
+            pair(j, 2 * (g // 2)),
+            NT,
+            preferred_element_type=F32,
+        )
+        sc_l[h, j] = scores
+        mx[h] = jnp.maximum(mx[h], fold(jnp.maximum, scores))
+
+    def long_mix(g, h, j):
+        top = mx[h]
+        weights = jnp.exp2(sc_l[h, j] * SCALE - jnp.concatenate([top] * 6, axis=1))
+        tot[h] += fold(jnp.add, weights)
+        acc[h] += jnp.dot(
+            weights.astype(BF16), pair(j, 2 * (g // 2) + 1), preferred_element_type=F32
+        )
 
     def long_attention(g):
-        kv = g // 2
         length = len_ref[0]
-        q2[pl.ds(0, LONG), :] = qb[g, pl.ds(SEQ, LONG), pl.ds(0, HD)]
-        q2[pl.ds(LONG, LONG), :] = qb[g, pl.ds(SEQ, LONG), pl.ds(HD, HD)]
         mx[...] = jnp.full_like(mx, HIDDEN)
         tot[...] = jnp.zeros_like(tot)
         acc[...] = jnp.zeros_like(acc)
 
-        @pl.loop(0, blk)
+        def row_bias(j):
+            key_pos = j * (2 * LONG) + lax.broadcasted_iota(jnp.int32, (1, 2 * LONG), 1)
+            return jnp.where(key_pos < length, 0.0, HIDDEN)
+
+        def top(h):
+            mx[h] = jnp.broadcast_to(jnp.max(mx[h], axis=1, keepdims=True) * SCALE, (LONG, HD))
+
+        def finish(h):
+            query_pos = blk * LONG + lax.broadcasted_iota(jnp.int32, (LONG, HD), 0)
+            mixed = acc[h] / jnp.sum(tot[h], axis=1, keepdims=True)
+            lob[g, :, pl.ds(h * HD, HD)] = jnp.where(query_pos < length, mixed, 0.0).astype(BF16)
+
+        @pl.loop(0, cx)
         def _(j):
-            key_pos = j * LONG + lax.broadcasted_iota(jnp.int32, (1, LONG), 1)
-            long_step(kv, j, jnp.where(key_pos < length, 0.0, HIDDEN), False)
-
-        diagonal = bias_l[...]
-        long_step(kv, blk, jnp.concatenate([diagonal, diagonal], axis=0), False)
-        query_pos = blk * LONG + lax.broadcasted_iota(jnp.int32, (LONG, HD), 0)
-        for h in range(2):
-            half = pl.ds(h * LONG, LONG)
-            mixed = acc[half, :] / tot[half, :]
-            lob[g, :, pl.ds(h * HD, HD)] = jnp.where(query_pos < length, mixed, 0.0).astype(BF16)
+            long_score(g, 0, j, row_bias(j))
+
+        long_score(g, 0, cx, bias_l[...])
+        top(0)
+
+        @pl.loop(0, cx)
+        def _(j):
+            long_score(g, 1, j, row_bias(j))
+            long_mix(g, 0, j)
+
+        long_score(g, 1, cx, bias_l[...])
+        long_mix(g, 0, cx)
+        top(1)
+        finish(0)
+
+        @pl.loop(0, cx + 1)
+        def _(j):
+            long_mix(g, 1, j)
+
+        finish(1)
 
     outs = []
     peer_outs = []
@@ -393,11 +446,12 @@
             pltpu.VMEM((4, SEQ, WIDTH), BF16),
             pltpu.VMEM((4, LONG, WIDTH), BF16),
             pltpu.VMEM((SEQ, 768), F32),
-            pltpu.VMEM((LONG, LONG), F32),
-            pltpu.VMEM((2 * LONG, HD), BF16),
-            pltpu.VMEM((2 * LONG, HD), F32),
-            pltpu.VMEM((2 * LONG, 1), F32),
-            pltpu.VMEM((2 * LONG, 1), F32),
+            pltpu.VMEM((LONG, 2 * LONG), F32),
+            pltpu.VMEM((2, 256, 768), F32),
+            pltpu.VMEM((2, 4, LONG, 2 * LONG), F32),
+            pltpu.VMEM((2, LONG, HD), F32),
+            pltpu.VMEM((2, LONG, HD), F32),
+            pltpu.VMEM((2, LONG, HD), F32),
             dma((13, 3, 4)),
             dma((13, 3, 4)),
             dma((10,)),
@@ -409,7 +463,7 @@
             dma((8,)),
         ],
         compiler_params=pltpu.CompilerParams(
-            collective_id=0, has_side_effects=True, vmem_limit_bytes=63_000_000
+            collective_id=0, has_side_effects=True, vmem_limit_bytes=60_000_000
         ),
     )(short_tokens, short_segments, long_tokens, long_lengths, w_query, w_key, w_value)
 

time: 177 us -> 130 us (0.73)
  the two profiles are of different devices: /device:TPU:14 before, /device:TPU:6 now
where the time goes in v2:
time: 130 us; the launch traced here: 129 us
  Pallas kernels  124 us (95%)
  local copies, waits for them, and re-layouts  4.12 us (3%)
    pallas_call x1, Pallas kernels, local(): pl.pallas_call(kernel, out_shape=(jax.ShapeDtypeStruct((1, HALF, 2 * SEQ)...  124 us
    unnamed x4, local copies, waits for them, and re-layouts  4.12 us

profile of v2, /device:TPU:6, one launch (start us, length us, event | category | flops | bytes accessed | tf_op | source)
XLA Modules:
  0.0 129.1 jit_solution(2222038891400072615)
XLA Ops:
  1.3 123.7 %shard_map.86 = (bf16[1,512,2048]{2,1,0:T(8,128)(2,1)}, bf16[1,384,1024]{2,1,0:T(8,128)(2,1)}) custom-call(bf16[1,512,4096]{2,1,0:T(8,128)(2,1)} %xs_hbm.1, s32[1,1024]{1,0:T(1,128)} %seg_ref.1, bf16[1,384,4096]{2,1,0:T(8,128)(2,1)} %xl_hbm.1, s32[1]{0:T(128)S(6)} %copy.11.len_ref, bf16[64,1024]{1,0:T(8,128)(2,1)} %wq_hbm.1, bf16[64,256]{1,0:T(8,128)(2,1)} %wk_hbm.1, ...), custom_call_target="tpu_custom_call" | custom-call | tf_op jit(solution)/shard_map/pallas_call | solution.py:431
  125.0 0.0 copy-start
  125.0 3.2 %copy.12 = bf16[1,512,2048]{2,1,0:T(8,128)(2,1)} copy(bf16[1,512,2048]{2,1,0:T(8,128)(2,1)} %get-tuple-element.4) | data formatting | bytes 4194304
  128.2 0.0 copy-done
  128.2 0.9 copy.13
Async XLA Ops:
  125.0 3.2 %copy-start = (bf16[1,384,1024]{2,1,0:T(8,128)(2,1)S(1)}, bf16[1,384,1024]{2,1,0:T(8,128)(2,1)}, u32[]{:S(2)}) copy-start(bf16[1,384,1024]{2,1,0:T(8,128)(2,1)} %get-tuple-element.5) | copy-start | bytes 2359300

commit v3 on v1

v3 whole, which is shorter than its diff:
```python
import math

import jax
import jax.numpy as jnp
from jax import lax
from jax.experimental import pallas as pl
from jax.experimental.pallas import tpu as pltpu
from jax.sharding import PartitionSpec as P

MESH = pl.DeviceIdType.MESH
BF16 = jnp.bfloat16
F32 = jnp.float32
HD = 128
D = 4096
SEQ = 1024
HALF = 512
LONG = 384
ROWS = SEQ + LONG
TILE = ROWS // 2
GROUPS = 6
WIDTH = 256
HIDDEN = -1e30
VMEM = 60_000_000
SCALE = math.log2(math.e) / math.sqrt(HD)

ORDERS = ("xyz", "yzx", "zxy")
PARTS = (
    ((0, 32), (32, 16), (48, 16)),
    ((0, 16), (16, 16), (32, 32)),
    ((0, 32), (32, 16), (48, 16)),
    ((0, 32), (32, 16), (48, 16)),
    ((0, 16), (16, 32), (48, 16)),
    ((0, 16), (16, 32), (48, 16)),
)
FIRST = ((0,), (1,), (2, 3), (4, 5),)
ORDER = (
    "P0a01", "P0a02", "P0a00", "P0a20", "P0a21", "P0a12", "P0a11", "P0a42", "P0a10", "P0a40", "B", "P0a41", "P0a22",
    "P0b02", "P0b01", "P0b00", "P0b12", "P0b21", "P0b11", "P0b42", "P0b20", "P0b10", "P0b22", "P0b41", "P0b40",
    "P1a02", "P1a01", "P1a00", "P1a12", "P1a21", "P1a31", "P1a11", "P1a52", "P1a42", "P1a22", "P1a30", "P1a32",
    "P1a10", "P1a41", "P1a40", "P1b02", "P1b01", "P1b21", "P1b00", "P1b12", "P1b31", "P1a51", "P1b11", "P1b52",
    "P1a50", "P1b30", "P1b42", "P1b10", "P1b41", "P1b22", "P1b40", "P2a01", "P2a21", "P1b32", "P1a20", "P2a00",
    "P2a31", "P2a02", "P1b50", "P2a12", "P2a10", "P2a11", "P2a41", "P2a42", "P2a40", "P2b01", "P1b20", "P2b02",
    "P2b21", "P2a32", "P2b00", "P2b31", "P2b10", "P2b12", "P2a30", "P2b11", "P2b40", "P2b42", "P2a22", "P2a20",
    "P2b41", "P2b32", "W0", "X", "pr01", "K2", "K1", "pr00", "P2b30", "W1", "pr11", "V1", "V2", "pr10", "P2b22",
    "W4", "pr4", "P2b20", "sh2", "P1b51", "K3", "W3", "pr3", "V4", "V3", "P2a50", "sh1", "W2", "P2a51", "lo1own",
    "K5", "lo2own", "pr2", "P2b50", "V5", "sh0", "K4", "lo0own", "P2b51", "lo0near", "P2a52", "lo0far", "lo2near",
    "lo2far", "lo1near", "lo0other", "P2b52", "lo2other", "lo1far", "lo1other", "W5", "pr5", "sh3", "lo3own",
    "lo3near", "lo3far", "lo3other",
)

NT = (((1,), (1,)), ((), ()))


def kernel(
    xs_hbm, seg_ref, xl_hbm, len_ref, wq_hbm, wk_hbm, wv_hbm,
    so_hbm, lo_hbm,
    w, x, kb, vb, qb, kvl, sob, lob, bias_s, bias_l, sc_s, sc_l, acc, mx, tot,
    send_sem, recv_sem, kv_send, kv_recv, x_sem, own_sem, out_send, out_recv, out_own,
):
    blk, core, dp = lax.axis_index("blk"), lax.axis_index("uly"), lax.axis_index("dp")
    cx, yl = blk // 2, blk % 2
    cz, yh = dp // 2, dp % 2
    cy = yh * 2 + yl
    here = {"x": cx, "y": cy, "z": cz}

    def device(dim, step):
        at = dict(here)
        at[dim] = (here[dim] + step + 4) % 4
        return (at["x"] * 2 + at["y"] % 2, core, at["z"] * 2 + at["y"] // 2)

    sibling = (blk, 1 - core, dp)

    own = [
        pltpu.make_async_copy(wk_hbm, w.at[0, cx, yl, cz, yh], own_sem.at[0]),
        pltpu.make_async_copy(wv_hbm, w.at[1, cx, yl, cz, yh], own_sem.at[1]),
    ]
    for g in range(4):
        own.append(
            pltpu.make_async_copy(
                wq_hbm.at[:, pl.ds(g * WIDTH, WIDTH)], w.at[2 + g, cx, yl, cz, yh], own_sem.at[2 + g]
            )
        )
    my_rows = pl.ds(pl.multiple_of(core * HALF, HALF), HALF)
    own_x = pltpu.make_async_copy(xs_hbm.at[0], x.at[my_rows], x_sem.at[0])
    own_l = pltpu.make_async_copy(xl_hbm.at[0], x.at[pl.ds(SEQ, LONG)], x_sem.at[1])
    for copy in own + [own_l, own_x]:
        copy.start()

    barrier = pltpu.get_barrier_semaphore()
    for dim in "xyz":
        for step in (1, -1):
            pl.semaphore_signal(barrier, inc=1, device_id=device(dim, step), device_id_type=MESH)
    pl.semaphore_signal(barrier, inc=1, device_id=sibling, device_id_type=MESH)
    pl.semaphore_wait(barrier, 7)

    peer_x = pltpu.make_async_remote_copy(
        src_ref=xs_hbm.at[0], dst_ref=x.at[my_rows], send_sem=x_sem.at[2], recv_sem=x_sem.at[3],
        device_id=sibling, device_id_type=MESH,
    )
    for copy in own:
        copy.wait()

    def block(groups, part, phase, position, half=None):
        first, count = PARTS[groups[0]][part]
        order = ORDERS[part]
        at = dict(here)
        at[order[phase]] = position
        done = order[:phase]
        ix = slice(None) if "x" in done else at["x"]
        iz = slice(None) if "z" in done else at["z"]
        il = slice(None) if "y" in done else at["y"] % 2
        ih = slice(None) if "y" in done else at["y"] // 2
        columns = slice(None)
        if half is not None:
            if phase == 0:
                columns = pl.ds(half * 128, 128)
            elif order[0] == "x":
                ix = pl.ds(2 * half, 2)
            elif order[0] == "z":
                iz = pl.ds(2 * half, 2)
            else:
                il = half
        which = pl.ds(groups[0], len(groups)) if len(groups) > 1 else groups[0]
        return w.at[which, ix, il, iz, ih, pl.ds(first, count), columns]

    def hop(groups, part, phase, slot):
        dim = ORDERS[part][phase]
        step = 1 if slot % 2 == 0 else -1
        if slot < 2:
            ref = block(groups, part, phase, here[dim])
        else:
            ref = block(groups, part, phase, (here[dim] - step + 4) % 4, half=slot % 2)
        stage = phase * GROUPS + groups[0]
        return pltpu.make_async_remote_copy(
            src_ref=ref, dst_ref=ref,
            send_sem=send_sem.at[stage, part, slot], recv_sem=recv_sem.at[stage, part, slot],
            device_id=device(dim, step), device_id_type=MESH,
        )

    sent = []

    def start(copy):
        copy.start()
        sent.append(copy)

    def send(groups, part, phase, second):
        for slot in (2, 3) if second else (0, 1):
            start(hop(groups, part, phase, slot))

    def arrive(groups, part, phase, second):
        for slot in (2, 3) if second else (0, 1):
            hop(groups, part, phase, slot).wait_recv()

    near, far = (cx + 3) % 4, (cx + 1) % 4
    other = (cx + 2) % 4
    keys, vals = pl.ds(0, 2), pl.ds(2, 2)
    kv_table = (
        ("y", kvl.at[cx, yl, keys]),
        ("x+", kvl.at[cx, yl, keys]),
        ("x-", kvl.at[cx, yl, keys]),
        ("x+", kvl.at[cx, 1 - yl, keys]),
        ("x-", kvl.at[cx, 1 - yl, keys]),
        ("x+", kvl.at[near, yl, keys]),
        ("x-", kvl.at[far, 1 - yl, keys]),
        ("x+", kvl.at[cx, yl, vals]),
        ("x-", kvl.at[cx, yl, vals]),
        ("y", kvl.at[cx, yl, vals]),
        ("x+", kvl.at[near, yl, 2]),
        ("x-", kvl.at[far, yl, 3]),
        ("y", kvl.at[near, yl, vals]),
        ("y", kvl.at[far, yl, vals]),
        ("y", kvl.at[other, yl, vals]),
    )

    def kv_hop(index):
        way, ref = kv_table[index]
        to = (cx * 2 + 1 - yl, core, dp) if way == "y" else device("x", 1 if way == "x+" else -1)
        return pltpu.make_async_remote_copy(
            src_ref=ref, dst_ref=ref, send_sem=kv_send.at[index], recv_sem=kv_recv.at[index],
            device_id=to, device_id_type=MESH,
        )

    kv_steps = {
        "K1": ((0,), ()),
        "K2": ((1, 2), ()),
        "K3": ((3, 4), (0,)),
        "K4": ((5,), (1,)),
        "K5": ((6,), (4,)),
        "V1": ((7, 8), ()),
        "V2": ((9,), ()),
        "V3": ((10, 11), (7, 8)),
        "V4": ((12, 13), (7, 8)),
        "V5": ((14,), (10, 11)),
    }
    kv_needs = {"own": (0, 9), "near": (1, 3, 7, 12), "far": (2, 4, 8, 13), "other": (5, 6, 10, 11, 14)}
    arrived = set()

    def kv_wait(indices):
        for index in indices:
            if index not in arrived:
                arrived.add(index)
                kv_hop(index).wait_recv()

    def rows_of(g, rows):
        return jnp.dot(x[rows, :], w[g].reshape(D, WIDTH), preferred_element_type=F32).astype(BF16)

    def project_kv(g, tile):
        @pl.when(core < 2)
        def _():
            rows = pl.ds(tile * TILE, TILE)
            result = rows_of(g, rows)
            (kb, vb)[g][rows, :] = result
            if tile == 1:
                for h in range(2):
                    kvl[cx, yl, 2 * g + h] = result[SEQ - TILE :, h * HD : (h + 1) * HD]

    def project_q(g):
        @pl.loop(0, ROWS // TILE)
        def _(i):
            rows = pl.ds(pl.multiple_of(i * TILE, 64), TILE)
            qb[g, rows, :] = rows_of(g + 2, rows)

    def short_bias():
        @pl.loop(0, 8)
        def _(i):
            first = pl.multiple_of(i * 128, 128)
            own_seg = seg_ref[:, pl.ds(first, 128)].astype(F32)
            query_seg = jnp.transpose(jnp.broadcast_to(own_seg, (128, 128)))
            window = jnp.maximum(i // 2 - 2, 0) * 256
            for j in range(6):
                start = pl.multiple_of(window + j * 128, 128)
                key_seg = jnp.broadcast_to(seg_ref[:, pl.ds(start, 128)].astype(F32), (128, 128))
                query_pos = first + lax.broadcasted_iota(jnp.int32, (128, 128), 0)
                key_pos = start + lax.broadcasted_iota(jnp.int32, (128, 128), 1)
                visible = (key_pos <= query_pos) & (key_seg == query_seg)
                bias_s[pl.ds(first, 128), pl.ds(j * 128, 128)] = jnp.where(visible, 0.0, HIDDEN)

    def long_bias():
        query_pos = yl * LONG + lax.broadcasted_iota(jnp.int32, (LONG, 2 * LONG), 0)
        key_pos = lax.broadcasted_iota(jnp.int32, (LONG, 2 * LONG), 1)
        visible = (key_pos <= query_pos) & (key_pos + cx * (2 * LONG) < len_ref[0])
        bias_l[...] = jnp.where(visible, 0.0, HIDDEN)

    def short_attention(g):
        kv = pl.ds((g // 2) * HD, HD)

        @pl.loop(0, 2)
        def _(h):
            head = pl.ds(pl.multiple_of(h * HD, HD), HD)

            def score(i):
                width = 256 * min(i + 1, 3)
                sc_s[i % 2, :, pl.ds(0, width)] = lax.dot_general(
                    qb[g, pl.ds(i * 256, 256), head],
                    kb[pl.ds(max(i - 2, 0) * 256, width), kv],
                    NT,
                    preferred_element_type=F32,
                )

            score(0)
            for i in range(4):
                if i < 3:
                    score(i + 1)
                width = 256 * min(i + 1, 3)
                rows = pl.ds(i * 256, 256)
                scores = sc_s[i % 2, :, pl.ds(0, width)] * SCALE + bias_s[rows, pl.ds(0, width)]
                top = jnp.max(scores, axis=1, keepdims=True)
                weights = jnp.exp2(scores - top)
                total = jnp.sum(weights, axis=1, keepdims=True)
                mixed = jnp.dot(
                    weights.astype(BF16),
                    vb[pl.ds(max(i - 2, 0) * 256, width), kv],
                    preferred_element_type=F32,
                )
                sob[g, rows, head] = (mixed / total).astype(BF16)

    def tiles(value):
        return [value[:, t * HD : (t + 1) * HD] for t in range(value.shape[1] // HD)]

    def fold(op, value):
        parts = tiles(value)
        while len(parts) > 1:
            parts = [
                op(parts[n], parts[n + 1]) if n + 1 < len(parts) else parts[n]
                for n in range(0, len(parts), 2)
            ]
        return parts[0]

    def pair(j, which):
        return jnp.concatenate([kvl[j, 0, which], kvl[j, 1, which]], axis=0)

    def long_part(g, j, bias, fresh):
        kv = g // 2
        for h in range(2):
            sc_l[h] = bias + lax.dot_general(
                qb[g, pl.ds(SEQ, LONG), pl.ds(h * HD, HD)], pair(j, kv), NT, preferred_element_type=F32
            )
        for h in range(2):
            n = 2 * g + h
            largest = jnp.max(fold(jnp.maximum, sc_l[h]), axis=1, keepdims=True) * SCALE
            top = jnp.broadcast_to(largest, (LONG, HD))
            if not fresh:
                top = jnp.maximum(mx[n], top)
            weights = jnp.exp2(sc_l[h] * SCALE - jnp.concatenate([top] * 6, axis=1))
            mixed = jnp.dot(weights.astype(BF16), pair(j, 2 + kv), preferred_element_type=F32)
            if fresh:
                tot[n] = fold(jnp.add, weights)
                acc[n] = mixed
            else:
                shrink = jnp.exp2(mx[n] - top)
                tot[n] = tot[n] * shrink + fold(jnp.add, weights)
                acc[n] = acc[n] * shrink + mixed
            mx[n] = top

    def long_own(g):
        long_part(g, cx, bias_l[...], True)

    def long_before(g, j):
        @pl.when(j < cx)
        def _():
            key_pos = j * (2 * LONG) + lax.broadcasted_iota(jnp.int32, (1, 2 * LONG), 1)
            long_part(g, j, jnp.where(key_pos < len_ref[0], 0.0, HIDDEN), False)

    def long_finish(g):
        query_pos = blk * LONG + lax.broadcasted_iota(jnp.int32, (LONG, HD), 0)
        for h in range(2):
            mixed = acc[2 * g + h] / jnp.sum(tot[2 * g + h], axis=1, keepdims=True)
            mixed = jnp.where(query_pos < len_ref[0], mixed, 0.0)
            lob[g, :, pl.ds(h * HD, HD)] = mixed.astype(BF16)

    outs = []
    peer_outs = []

    def ship_short(g):
        columns = pl.ds(pl.multiple_of(core * SEQ + g * WIDTH, WIDTH), WIDTH)
        theirs = pl.ds(pl.multiple_of((1 - core) * HALF, HALF), HALF)
        peer = pltpu.make_async_remote_copy(
            src_ref=sob.at[g, theirs], dst_ref=so_hbm.at[0, :, columns],
            send_sem=out_send.at[g], recv_sem=out_recv.at[g], device_id=sibling, device_id_type=MESH,
        )
        mine = pltpu.make_async_copy(sob.at[g, my_rows], so_hbm.at[0, :, columns], out_own.at[g])
        peer.start()
        mine.start()
        peer_outs.append(peer)
        outs.append(mine)

    def ship_long(g):
        mine = pltpu.make_async_copy(
            lob.at[g], lo_hbm.at[0, :, pl.ds(g * WIDTH, WIDTH)], out_own.at[4 + g]
        )
        mine.start()
        outs.append(mine)

    groups_of = {g: groups for groups in FIRST for g in groups}
    parts_of = [[p for p in range(3) if PARTS[g][p][1]] for g in range(GROUPS)]

    def step(name):
        kind, rest = name[:2], name[2:]
        if kind[0] == "P":
            phase, second, g, part = int(kind[1]), rest[0] == "b", int(rest[1]), int(rest[2])
            groups = groups_of[g] if phase == 0 else (g,)
            if second:
                arrive(groups, part, phase, False)
            elif phase == 1:
                arrive_first(g, part)
            elif phase == 2:
                arrive(groups, part, 1, True)
            send(groups, part, phase, second)
        elif kind[0] in "KV":
            sends, needs = kv_steps[name]
            kv_wait(needs)
            for index in sends:
                start(kv_hop(index))
        elif kind[0] == "W":
            g = int(kind[1])
            for part in parts_of[g]:
                arrive((g,), part, 2, True)
        elif kind == "pr":
            if len(rest) == 2:
                project_kv(int(rest[0]), int(rest[1]))
            else:
                project_q(int(rest) - 2)
        elif kind == "sh":
            short_attention(int(rest))
            ship_short(int(rest))
        elif kind == "lo":
            g, which = int(rest[0]), rest[1:]
            kv_wait(kv_needs[which])
            if which == "own":
                long_own(g)
            else:
                long_before(g, {"near": near, "far": far, "other": other}[which])
            if which == "other":
                long_finish(g)
                ship_long(g)
        elif name == "X":
            own_x.wait()
            own_l.wait()
            peer_x.wait_recv()
        else:
            peer_x.start()
            long_bias()
            short_bias()

    met = set()

    def arrive_first(g, part):
        groups = groups_of[g]
        if (groups, part) not in met:
            met.add((groups, part))
            arrive(groups, part, 0, True)

    for name in ORDER:
        step(name)

    peer_x.wait_send()
    for copy in sent:
        copy.wait_send()
    for copy in outs:
        copy.wait()
    for copy in peer_outs:
        copy.wait()


def local(short_tokens, short_segments, long_tokens, long_lengths, w_query, w_key, w_value):
    anywhere = pl.BlockSpec(memory_space=pl.ANY)
    vmem = pl.BlockSpec(memory_space=pltpu.VMEM)
    smem = pl.BlockSpec(memory_space=pltpu.SMEM)
    dma = pltpu.SemaphoreType.DMA
    return pl.pallas_call(
        kernel,
        out_shape=(
            jax.ShapeDtypeStruct((1, HALF, 2 * SEQ), BF16),
            jax.ShapeDtypeStruct((1, LONG, SEQ), BF16),
        ),
        in_specs=[anywhere, vmem, anywhere, smem, anywhere, anywhere, anywhere],
        out_specs=(anywhere, anywhere),
        scratch_shapes=[
            pltpu.VMEM((GROUPS, 4, 2, 4, 2, 64, WIDTH), BF16),
            pltpu.VMEM((ROWS, D), BF16),
            pltpu.VMEM((ROWS, WIDTH), BF16),
            pltpu.VMEM((ROWS, WIDTH), BF16),
            pltpu.VMEM((4, ROWS, WIDTH), BF16),
            pltpu.VMEM((4, 2, 4, LONG, HD), BF16),
            pltpu.VMEM((4, SEQ, WIDTH), BF16),
            pltpu.VMEM((4, LONG, WIDTH), BF16),
            pltpu.VMEM((SEQ, 768), F32),
            pltpu.VMEM((LONG, 2 * LONG), F32),
            pltpu.VMEM((2, 256, 768), F32),
            pltpu.VMEM((2, LONG, 2 * LONG), F32),
            pltpu.VMEM((8, LONG, HD), F32),
            pltpu.VMEM((8, LONG, HD), F32),
            pltpu.VMEM((8, LONG, HD), F32),
            dma((18, 3, 4)),
            dma((18, 3, 4)),
            dma((15,)),
            dma((15,)),
            dma((4,)),
            dma((6,)),
            dma((4,)),
            dma((4,)),
            dma((8,)),
        ],
        compiler_params=pltpu.CompilerParams(
            collective_id=0, has_side_effects=True, vmem_limit_bytes=VMEM
        ),
    )(short_tokens, short_segments, long_tokens, long_lengths, w_query, w_key, w_value)


def solution(mesh):
    return jax.shard_map(
        local,
        mesh=mesh,
        in_specs=(
            P(("blk", "dp"), "uly", None),
            P(("blk", "dp"), None),
            P("dp", "blk", None),
            P("dp"),
            P(("blk", "dp"), "uly"),
            P(("blk", "dp"), "uly"),
            P(("blk", "dp"), "uly"),
        ),
        out_specs=(P(("blk", "dp"), "uly", None), P("dp", "blk", "uly")),
        check_vma=False,
    )
```

time: 177 us -> 102 us (0.58)
  the two profiles are of different devices: /device:TPU:14 before, /device:TPU:6 now
where the time goes in v3:
time: 102 us
  Pallas kernels  96.3 us (94%)
  local copies, waits for them, and re-layouts  4.12 us (4%)
  between operations  1.29 us (1%)
    pallas_call x1, Pallas kernels, local(): pl.pallas_call(kernel, out_shape=(jax.ShapeDtypeStruct((1, HALF, 2 * SEQ)...  96.3 us
    unnamed x4, local copies, waits for them, and re-layouts  4.12 us

profile of v3, /device:TPU:6, one launch (start us, length us, event | category | flops | bytes accessed | tf_op | source)
XLA Modules:
  0.0 101.7 jit_solution(8989072954072226308)
XLA Ops:
  1.3 96.3 %shard_map.86 = (bf16[1,512,2048]{2,1,0:T(8,128)(2,1)}, bf16[1,384,1024]{2,1,0:T(8,128)(2,1)}) custom-call(bf16[1,512,4096]{2,1,0:T(8,128)(2,1)} %xs_hbm.1, s32[1,1024]{1,0:T(1,128)} %seg_ref.1, bf16[1,384,4096]{2,1,0:T(8,128)(2,1)} %xl_hbm.1, s32[1]{0:T(128)S(6)} %copy.11.len_ref, bf16[64,1024]{1,0:T(8,128)(2,1)} %wq_hbm.1, bf16[64,256]{1,0:T(8,128)(2,1)} %wk_hbm.1, ...), custom_call_target="tpu_custom_call" | custom-call | tf_op jit(solution)/shard_map/pallas_call | solution.py:430
  97.6 0.0 copy-start
  97.6 3.2 %copy.12 = bf16[1,512,2048]{2,1,0:T(8,128)(2,1)} copy(bf16[1,512,2048]{2,1,0:T(8,128)(2,1)} %get-tuple-element.4) | data formatting | bytes 4194304
  100.8 0.0 copy-done
  100.8 0.9 copy.13
Async XLA Ops:
  97.6 3.2 %copy-start = (bf16[1,384,1024]{2,1,0:T(8,128)(2,1)S(1)}, bf16[1,384,1024]{2,1,0:T(8,128)(2,1)}, u32[]{:S(2)}) copy-start(bf16[1,384,1024]{2,1,0:T(8,128)(2,1)} %get-tuple-element.5) | copy-start | bytes 2359300

commit v4 on v3

--- a/solution.py
+++ b/solution.py
@@ -20,6 +20,7 @@
 GROUPS = 6
 WIDTH = 256
 HIDDEN = -1e30
+POOL = 40
 VMEM = 60_000_000
 SCALE = math.log2(math.e) / math.sqrt(HD)
 
@@ -42,10 +43,9 @@
     "P2a31", "P2a02", "P1b50", "P2a12", "P2a10", "P2a11", "P2a41", "P2a42", "P2a40", "P2b01", "P1b20", "P2b02",
     "P2b21", "P2a32", "P2b00", "P2b31", "P2b10", "P2b12", "P2a30", "P2b11", "P2b40", "P2b42", "P2a22", "P2a20",
     "P2b41", "P2b32", "W0", "X", "pr01", "K2", "K1", "pr00", "P2b30", "W1", "pr11", "V1", "V2", "pr10", "P2b22",
-    "W4", "pr4", "P2b20", "sh2", "P1b51", "K3", "W3", "pr3", "V4", "V3", "P2a50", "sh1", "W2", "P2a51", "lo1own",
-    "K5", "lo2own", "pr2", "P2b50", "V5", "sh0", "K4", "lo0own", "P2b51", "lo0near", "P2a52", "lo0far", "lo2near",
-    "lo2far", "lo1near", "lo0other", "P2b52", "lo2other", "lo1far", "lo1other", "W5", "pr5", "sh3", "lo3own",
-    "lo3near", "lo3far", "lo3other",
+    "W4", "pr4", "P2b20", "sh2", "P1b51", "K3", "W3", "pr3", "V4", "V3", "P2a50", "sh1", "W2", "P2a51", "lo1o",
+    "K5", "lo2o", "pr2", "P2b50", "V5", "sh0", "K4", "lo0o", "P2b51", "P2a52", "lo0nf", "lo2nf", "lo0t", "P2b52",
+    "lo2t", "lo1nft", "W5", "pr5", "sh3", "lo3onft",
 )
 
 NT = (((1,), (1,)), ((), ()))
@@ -100,17 +100,21 @@
     for copy in own:
         copy.wait()
 
-    def block(groups, part, phase, position, half=None):
+    def block(groups, part, phase, position, half=None, both=False):
         first, count = PARTS[groups[0]][part]
         order = ORDERS[part]
+        dim = order[phase]
         at = dict(here)
-        at[order[phase]] = position
+        at[dim] = position
         done = order[:phase]
         ix = slice(None) if "x" in done else at["x"]
         iz = slice(None) if "z" in done else at["z"]
         il = slice(None) if "y" in done else at["y"] % 2
         ih = slice(None) if "y" in done else at["y"] // 2
         columns = slice(None)
+        if both:
+            two = pl.ds(0, 2)
+            ix, il, iz = two if dim == "x" else ix, two if dim == "y" else il, two if dim == "z" else iz
         if half is not None:
             if phase == 0:
                 columns = pl.ds(half * 128, 128)
@@ -123,33 +127,49 @@
         which = pl.ds(groups[0], len(groups)) if len(groups) > 1 else groups[0]
         return w.at[which, ix, il, iz, ih, pl.ds(first, count), columns]
 
-    def hop(groups, part, phase, slot):
+    stage_of = {}
+    sent = []
+    held = [None] * POOL
+
+    def stage(groups, part, phase, second):
+        return stage_of.setdefault((groups, part, phase, second), len(stage_of))
+
+    def remote(ref, to, send_ref, recv_ref):
+        return pltpu.make_async_remote_copy(
+            src_ref=ref, dst_ref=ref, send_sem=send_ref, recv_sem=recv_ref, device_id=to, device_id_type=MESH
+        )
+
+    def whole(groups, part, phase, second, slot):
         dim = ORDERS[part][phase]
-        step = 1 if slot % 2 == 0 else -1
-        if slot < 2:
-            ref = block(groups, part, phase, here[dim])
-        else:
-            ref = block(groups, part, phase, (here[dim] - step + 4) % 4, half=slot % 2)
-        stage = phase * GROUPS + groups[0]
-        return pltpu.make_async_remote_copy(
-            src_ref=ref, dst_ref=ref,
-            send_sem=send_sem.at[stage, part, slot], recv_sem=recv_sem.at[stage, part, slot],
-            device_id=device(dim, step), device_id_type=MESH,
+        ref = block(groups, part, phase, here[dim], both=not second)
+        return remote(
+            ref, device(dim, 1), send_sem.at[slot], recv_sem.at[stage(groups, part, phase, second)]
         )
 
-    sent = []
+    def send(groups, part, phase, second):
+        slot = len(sent) % POOL
+        if held[slot] is not None:
+            held[slot].wait_send()
+        dim = ORDERS[part][phase]
+        for k, way in enumerate((1, -1)):
+            if second:
+                ref = block(groups, part, phase, (here[dim] - way + 4) % 4, half=k)
+            else:
+                ref = block(groups, part, phase, here[dim])
+            remote(
+                ref, device(dim, way), send_sem.at[slot], recv_sem.at[stage(groups, part, phase, second)]
+            ).start()
+        held[slot] = whole(groups, part, phase, second, slot)
+        sent.append(slot)
+
+    def arrive(groups, part, phase, second):
+        whole(groups, part, phase, second, 0).wait_recv()
+
+    kv_sent = []
 
     def start(copy):
         copy.start()
-        sent.append(copy)
-
-    def send(groups, part, phase, second):
-        for slot in (2, 3) if second else (0, 1):
-            start(hop(groups, part, phase, slot))
-
-    def arrive(groups, part, phase, second):
-        for slot in (2, 3) if second else (0, 1):
-            hop(groups, part, phase, slot).wait_recv()
+        kv_sent.append(copy)
 
     near, far = (cx + 3) % 4, (cx + 1) % 4
     other = (cx + 2) % 4
@@ -289,21 +309,36 @@
     def pair(j, which):
         return jnp.concatenate([kvl[j, 0, which], kvl[j, 1, which]], axis=0)
 
-    def long_part(g, j, bias, fresh):
+    def long_parts(g, parts):
         kv = g // 2
-        for h in range(2):
-            sc_l[h] = bias + lax.dot_general(
+        where = {"own": cx, "near": near, "far": far, "other": other}
+        units = [(name, h) for name in parts for h in range(2)]
+
+        def score(n):
+            name, h = units[n]
+            j = where[name]
+            if name == "own":
+                bias = bias_l[...]
+            else:
+                key_pos = j * (2 * LONG) + lax.broadcasted_iota(jnp.int32, (1, 2 * LONG), 1)
+                bias = jnp.where((key_pos < len_ref[0]) & (j < cx), 0.0, HIDDEN)
+            sc_l[n % 2] = bias + lax.dot_general(
                 qb[g, pl.ds(SEQ, LONG), pl.ds(h * HD, HD)], pair(j, kv), NT, preferred_element_type=F32
             )
-        for h in range(2):
+
+        score(0)
+        for i, (name, h) in enumerate(units):
+            if i + 1 < len(units):
+                score(i + 1)
             n = 2 * g + h
-            largest = jnp.max(fold(jnp.maximum, sc_l[h]), axis=1, keepdims=True) * SCALE
+            scores = sc_l[i % 2]
+            largest = jnp.max(fold(jnp.maximum, scores), axis=1, keepdims=True) * SCALE
             top = jnp.broadcast_to(largest, (LONG, HD))
-            if not fresh:
+            if name != "own":
                 top = jnp.maximum(mx[n], top)
-            weights = jnp.exp2(sc_l[h] * SCALE - jnp.concatenate([top] * 6, axis=1))
-            mixed = jnp.dot(weights.astype(BF16), pair(j, 2 + kv), preferred_element_type=F32)
-            if fresh:
+            weights = jnp.exp2(scores * SCALE - jnp.concatenate([top] * 6, axis=1))
+            mixed = jnp.dot(weights.astype(BF16), pair(where[name], 2 + kv), preferred_element_type=F32)
+            if name == "own":
                 tot[n] = fold(jnp.add, weights)
                 acc[n] = mixed
             else:
@@ -311,15 +346,6 @@
                 tot[n] = tot[n] * shrink + fold(jnp.add, weights)
                 acc[n] = acc[n] * shrink + mixed
             mx[n] = top
-
-    def long_own(g):
-        long_part(g, cx, bias_l[...], True)
-
-    def long_before(g, j):
-        @pl.when(j < cx)
-        def _():
-            key_pos = j * (2 * LONG) + lax.broadcasted_iota(jnp.int32, (1, 2 * LONG), 1)
-            long_part(g, j, jnp.where(key_pos < len_ref[0], 0.0, HIDDEN), False)
 
     def long_finish(g):
         query_pos = blk * LONG + lax.broadcasted_iota(jnp.int32, (LONG, HD), 0)
@@ -384,13 +410,13 @@
             short_attention(int(rest))
             ship_short(int(rest))
         elif kind == "lo":
-            g, which = int(rest[0]), rest[1:]
-            kv_wait(kv_needs[which])
-            if which == "own":
-                long_own(g)
-            else:
-                long_before(g, {"near": near, "far": far, "other": other}[which])
-            if which == "other":
+            g = int(rest[0])
+            names = {"o": "own", "n": "near", "f": "far", "t": "other"}
+            parts = [names[letter] for letter in rest[1:]]
+            for part in parts:
+                kv_wait(kv_needs[part])
+            long_parts(g, parts)
+            if parts[-1] == "other":
                 long_finish(g)
                 ship_long(g)
         elif name == "X":
@@ -414,7 +440,7 @@
         step(name)
 
     peer_x.wait_send()
-    for copy in sent:
+    for copy in kv_sent + [copy for copy in held if copy is not None]:
         copy.wait_send()
     for copy in outs:
         copy.wait()
@@ -422,12 +448,31 @@
         copy.wait()
 
 
+def place(short_in, long_in, short_out, long_out, short_buf, long_buf, in_sem, out_sem):
+    pieces = [
+        (short_in.at[0, pl.ds(n * HALF // 4, HALF // 4)], short_buf.at[n], short_out.at[0, pl.ds(n * HALF // 4, HALF // 4)])
+        for n in range(4)
+    ] + [
+        (long_in.at[0, pl.ds(n * LONG // 2, LONG // 2)], long_buf.at[n], long_out.at[0, pl.ds(n * LONG // 2, LONG // 2)])
+        for n in range(2)
+    ]
+    fetches = [pltpu.make_async_copy(src, buf, in_sem.at[n]) for n, (src, buf, _) in enumerate(pieces)]
+    stores = [pltpu.make_async_copy(buf, dst, out_sem.at[n]) for n, (_, buf, dst) in enumerate(pieces)]
+    for copy in fetches:
+        copy.start()
+    for fetch, store in zip(fetches, stores):
+        fetch.wait()
+        store.start()
+    for copy in stores:
+        copy.wait()
+
+
 def local(short_tokens, short_segments, long_tokens, long_lengths, w_query, w_key, w_value):
     anywhere = pl.BlockSpec(memory_space=pl.ANY)
     vmem = pl.BlockSpec(memory_space=pltpu.VMEM)
     smem = pl.BlockSpec(memory_space=pltpu.SMEM)
     dma = pltpu.SemaphoreType.DMA
-    return pl.pallas_call(
+    shorts, longs = pl.pallas_call(
         kernel,
         out_shape=(
             jax.ShapeDtypeStruct((1, HALF, 2 * SEQ), BF16),
@@ -451,8 +496,8 @@
             pltpu.VMEM((8, LONG, HD), F32),
             pltpu.VMEM((8, LONG, HD), F32),
             pltpu.VMEM((8, LONG, HD), F32),
-            dma((18, 3, 4)),
-            dma((18, 3, 4)),
+            dma((POOL,)),
+            dma((6 * (2 * GROUPS + len(FIRST)),)),
             dma((15,)),
             dma((15,)),
             dma((4,)),
@@ -465,6 +510,21 @@
             collective_id=0, has_side_effects=True, vmem_limit_bytes=VMEM
         ),
     )(short_tokens, short_segments, long_tokens, long_lengths, w_query, w_key, w_value)
+    return pl.pallas_call(
+        place,
+        out_shape=(
+            jax.ShapeDtypeStruct(shorts.shape, BF16),
+            jax.ShapeDtypeStruct(longs.shape, BF16),
+        ),
+        in_specs=[anywhere, anywhere],
+        out_specs=(anywhere, anywhere),
+        scratch_shapes=[
+            pltpu.VMEM((4, HALF // 4, 2 * SEQ), BF16),
+            pltpu.VMEM((2, LONG // 2, SEQ), BF16),
+            dma((6,)),
+            dma((6,)),
+        ],
+    )(shorts, longs)
 
 
 def solution(mesh):

time: 102 us -> 96.3 us (0.944); the launches traced: 102 us -> 94.3 us
  local copies, waits for them, and re-layouts: 4.12 us -> 0 us
  Pallas kernels: 96.3 us -> 92.9 us
    pallas_call x1, Pallas kernels: 96.3 us -> 90.2 us  [local(): pl.pallas_call(kernel, out_shape=(jax.ShapeDtypeStruct((1, HALF, 2 * SEQ)...]
    unnamed x4 -> x0, local copies, waits for them, and re-layouts: 4.12 us -> none
    pallas_call x0 -> x1, Pallas kernels: none -> 2.71 us  [local(): pl.pallas_call(place, out_shape=(jax.ShapeDtypeStruct(shorts.shape, BF16)...]
where the time goes in v4:
time: 96.3 us; the launch traced here: 94.3 us
  Pallas kernels  92.9 us (96%)
  between operations  1.47 us (2%)
    pallas_call x1, Pallas kernels, local(): pl.pallas_call(kernel, out_shape=(jax.ShapeDtypeStruct((1, HALF, 2 * SEQ)...  90.2 us
    pallas_call x1, Pallas kernels, local(): pl.pallas_call(place, out_shape=(jax.ShapeDtypeStruct(shorts.shape, BF16)...  2.71 us

profile of v4, /device:TPU:6, one launch (start us, length us, event | category | flops | bytes accessed | tf_op | source)
XLA Modules:
  0.0 94.3 jit_solution(7494986923553036838)
XLA Ops:
  1.3 90.2 %shard_map.86 = (bf16[1,512,2048]{2,1,0:T(8,128)(2,1)}, bf16[1,384,1024]{2,1,0:T(8,128)(2,1)}) custom-call(bf16[1,512,4096]{2,1,0:T(8,128)(2,1)} %xs_hbm.1, s32[1,1024]{1,0:T(1,128)} %seg_ref.1, bf16[1,384,4096]{2,1,0:T(8,128)(2,1)} %xl_hbm.1, s32[1]{0:T(128)S(6)} %copy.9.len_ref, bf16[64,1024]{1,0:T(8,128)(2,1)} %wq_hbm.1, bf16[64,256]{1,0:T(8,128)(2,1)} %wk_hbm.1, ...), custom_call_target="tpu_custom_call" | custom-call | tf_op jit(solution)/shard_map/pallas_call | solution.py:475
  91.5 2.7 %shard_map.87 = (bf16[1,512,2048]{2,1,0:T(8,128)(2,1)}, bf16[1,384,1024]{2,1,0:T(8,128)(2,1)}) custom-call(bf16[1,512,2048]{2,1,0:T(8,128)(2,1)} %get-tuple-element.4.short_in, bf16[1,384,1024]{2,1,0:T(8,128)(2,1)} %get-tuple-element.5.long_in), custom_call_target="tpu_custom_call" | custom-call | tf_op jit(solution)/shard_map/pallas_call | solution.py:513

commit v5 on v4

--- a/solution.py
+++ b/solution.py
@@ -263,36 +263,34 @@
 
     def short_attention(g):
         kv = pl.ds((g // 2) * HD, HD)
-
-        @pl.loop(0, 2)
-        def _(h):
-            head = pl.ds(pl.multiple_of(h * HD, HD), HD)
-
-            def score(i):
-                width = 256 * min(i + 1, 3)
-                sc_s[i % 2, :, pl.ds(0, width)] = lax.dot_general(
-                    qb[g, pl.ds(i * 256, 256), head],
-                    kb[pl.ds(max(i - 2, 0) * 256, width), kv],
-                    NT,
-                    preferred_element_type=F32,
-                )
-
-            score(0)
-            for i in range(4):
-                if i < 3:
-                    score(i + 1)
-                width = 256 * min(i + 1, 3)
-                rows = pl.ds(i * 256, 256)
-                scores = sc_s[i % 2, :, pl.ds(0, width)] * SCALE + bias_s[rows, pl.ds(0, width)]
-                top = jnp.max(scores, axis=1, keepdims=True)
-                weights = jnp.exp2(scores - top)
-                total = jnp.sum(weights, axis=1, keepdims=True)
-                mixed = jnp.dot(
-                    weights.astype(BF16),
-                    vb[pl.ds(max(i - 2, 0) * 256, width), kv],
-                    preferred_element_type=F32,
-                )
-                sob[g, rows, head] = (mixed / total).astype(BF16)
+        items = [(i, h) for i in range(4) for h in range(2)]
+
+        def score(n):
+            i, h = items[n]
+            width = 256 * min(i + 1, 3)
+            sc_s[n % 2, :, pl.ds(0, width)] = lax.dot_general(
+                qb[g, pl.ds(i * 256, 256), pl.ds(h * HD, HD)],
+                kb[pl.ds(max(i - 2, 0) * 256, width), kv],
+                NT,
+                preferred_element_type=F32,
+            )
+
+        score(0)
+        for n, (i, h) in enumerate(items):
+            if n + 1 < len(items):
+                score(n + 1)
+            width = 256 * min(i + 1, 3)
+            rows = pl.ds(i * 256, 256)
+            scores = sc_s[n % 2, :, pl.ds(0, width)] * SCALE + bias_s[rows, pl.ds(0, width)]
+            top = jnp.max(scores, axis=1, keepdims=True)
+            weights = jnp.exp2(scores - top)
+            total = jnp.sum(weights, axis=1, keepdims=True)
+            mixed = jnp.dot(
+                weights.astype(BF16),
+                vb[pl.ds(max(i - 2, 0) * 256, width), kv],
+                preferred_element_type=F32,
+            )
+            sob[g, rows, pl.ds(h * HD, HD)] = (mixed / total).astype(BF16)
 
     def tiles(value):
         return [value[:, t * HD : (t + 1) * HD] for t in range(value.shape[1] // HD)]

time: 96.3 us -> 95.8 us (level)
  no operation moved by 1% of the time
where the time goes in v5:
time: 95.8 us; the launch traced here: 94 us
  Pallas kernels  92.5 us (97%)
  between operations  1.47 us (2%)
    pallas_call x1, Pallas kernels, local(): pl.pallas_call(kernel, out_shape=(jax.ShapeDtypeStruct((1, HALF, 2 * SEQ)...  89.8 us
    pallas_call x1, Pallas kernels, local(): pl.pallas_call(place, out_shape=(jax.ShapeDtypeStruct(shorts.shape, BF16)...  2.71 us

profile of v5, /device:TPU:6, one launch (start us, length us, event | category | flops | bytes accessed | tf_op | source)
XLA Modules:
  0.0 94.0 jit_solution(5030393447016546025)
XLA Ops:
  1.3 89.8 %shard_map.86 = (bf16[1,512,2048]{2,1,0:T(8,128)(2,1)}, bf16[1,384,1024]{2,1,0:T(8,128)(2,1)}) custom-call(bf16[1,512,4096]{2,1,0:T(8,128)(2,1)} %xs_hbm.1, s32[1,1024]{1,0:T(1,128)} %seg_ref.1, bf16[1,384,4096]{2,1,0:T(8,128)(2,1)} %xl_hbm.1, s32[1]{0:T(128)S(6)} %copy.9.len_ref, bf16[64,1024]{1,0:T(8,128)(2,1)} %wq_hbm.1, bf16[64,256]{1,0:T(8,128)(2,1)} %wk_hbm.1, ...), custom_call_target="tpu_custom_call" | custom-call | tf_op jit(solution)/shard_map/pallas_call | solution.py:473
  91.1 2.7 %shard_map.87 = (bf16[1,512,2048]{2,1,0:T(8,128)(2,1)}, bf16[1,384,1024]{2,1,0:T(8,128)(2,1)}) custom-call(bf16[1,512,2048]{2,1,0:T(8,128)(2,1)} %get-tuple-element.4.short_in, bf16[1,384,1024]{2,1,0:T(8,128)(2,1)} %get-tuple-element.5.long_in), custom_call_target="tpu_custom_call" | custom-call | tf_op jit(solution)/shard_map/pallas_call | solution.py:511
